TPU v7x, 32 devices: a whole 2x2x4 slice. The times are simulated.
32 devices in a mesh: pix: 8 (over z, y), rep: 4 (over x, core).
Axes of the slice: x: 2, y: 2, z: 4, core: 2. Of those that a mesh axis runs over, the one named last changes fastest.
Arguments:
- interferograms: float32 [256, 131072], P(('pix', 'rep')), may hold values from -6 to 6
- epoch_pairs: int32 [2, 256], replicated, may hold values from 0 to 63, as said below
- los: float32 [3, 131072], P(None, ('pix', 'rep')), may hold values from 0.3 to 1
- patch_place: int32 [2, 4096], replicated, may hold values from 0 to 255, as said below
- patch_depth: int32 [4096], replicated, may hold values from 0 to 7
Outputs:
- predicted: float32 [64, 131072], P(None, ('pix', 'rep'))
- slip: float32 [64, 4096], P(None, ('pix', 'rep'))
Inputs may be any that keep to these rules, and one draw needn't show every extreme that they name: `epoch_pairs`: row 0 holds an interferogram's earlier epoch and row 1 its later one; the two always differ. `patch_place`: row 0 is an east cell below 256; row 1 is a north cell below 32.
All inputs are finite; a program needn't handle non-finite values.
Results may differ from a plain program's by a relative error of at most 0.0037.
Values may be sent and summed in bfloat16 or wider, within the bound.
A program may use at most 64 MiB of HBM per device.

v0:
```python
import functools

import jax
import jax.numpy as jnp
from jax import lax
from jax.experimental import pallas as pl
from jax.experimental.pallas import tpu as pltpu
from jax.sharding import PartitionSpec as P

NEP = 64
IMG_W = 1024
LANES = 128

pixel_step = 0.1
patch_step = 0.4
damping = 0.5
depth_base = 0.5
depth_step = 0.25

F32 = jnp.float32
BF16 = jnp.bfloat16
NT = (((1,), (1,)), ((), ()))
EXTRA = 16


def kernel(
    cfg,
    pairs_ref,
    los_ref,
    place_ref,
    depth_ref,
    xs_ref,
    pred_ref,
    slip_ref,
    pcol_ref,
    prow_ref,
    mat,
    green,
    wacc,
    got,
    series,
    resid,
    bsend,
    bpart,
    send,
    part_a,
    part_b,
    gath_a,
    gath_b,
    full,
    guess,
    stage,
    xsend,
    own,
    half,
    pair_a,
    pair_b,
    s_x,
    r_x,
    r_in,
    s_b,
    r_b,
    s_p,
    r_pa,
    r_pb,
    s_h,
    r_ha,
    r_hb,
    s_g,
    r_ga,
    r_gb,
    s_f,
    r_fa,
    r_fb,
):
    n, reps, npix, npatch, parts, ifg_dev, lines, chunks = cfg
    me = lax.axis_index(("pix", "rep"))
    rep_size = lax.axis_size("rep")
    groups = npatch // LANES
    mine = me // reps
    gathered = n // reps
    split = reps == 1 and n % 8 == 0
    core = me % 2
    chip = me // 2
    partner = me + 1 - 2 * core
    batches = n // 8
    mesh_id = pl.DeviceIdType.MESH

    def ident(d):
        return {"pix": d // rep_size, "rep": d % rep_size}

    def settle(buf, count, sem):
        view = buf.at[pl.ds(0, count)]
        pltpu.make_async_copy(view, view, sem).wait()

    barrier = pltpu.get_barrier_semaphore()

    @pl.loop(1, n)
    def _(k):
        pl.semaphore_signal(
            barrier, inc=1, device_id=ident((me + k) % n), device_id_type=mesh_id
        )

    if chunks > 1:
        loads = r_in.shape[0]
        per_load = n // loads
        wide_load = per_load * npix
        span = npix // chunks
        for i in range(loads):
            pltpu.make_async_copy(
                xs_ref.at[:, pl.ds(i * wide_load, wide_load)],
                stage.at[:, pl.ds(i * wide_load, wide_load)],
                r_in.at[i],
            ).start()
        for i in range(loads):
            pltpu.make_async_copy(
                xs_ref.at[:, pl.ds(i * wide_load, wide_load)],
                stage.at[:, pl.ds(i * wide_load, wide_load)],
                r_in.at[i],
            ).wait()

            @pl.loop(0, per_load)
            def _(j):
                d = i * per_load + j
                for c in range(chunks):
                    at = pl.ds(pl.multiple_of(d * npix + c * span, span), span)
                    xsend[c, d, :, :] = stage[:, at].astype(BF16)

    pl.semaphore_wait(barrier, n - 1)

    for c in range(chunks):

        @pl.loop(1, n)
        def _(k):
            d = (me + k) % n
            pltpu.make_async_remote_copy(
                src_ref=xsend.at[c, d] if chunks > 1 else xs_ref.at[d],
                dst_ref=got.at[c, me],
                send_sem=s_x,
                recv_sem=r_x.at[c],
                device_id=ident(d),
                device_id_type=mesh_id,
            ).start()

    if chunks > 1:
        for c in range(chunks):
            got[c, me, :, :] = xsend[c, me, :, :]
    else:
        own_copy = pltpu.make_async_copy(xs_ref.at[me], got.at[0, me], r_in.at[0])
        own_copy.start()

    patch_x = (place_ref[0:1, :].astype(F32) + 0.5) * patch_step
    patch_y = (place_ref[1:2, :].astype(F32) + 0.5) * patch_step
    depth = depth_base + depth_step * depth_ref[...].astype(F32)
    scale = lax.rsqrt(depth)
    prow_ref[0:1, :] = patch_x
    prow_ref[1:2, :] = scale
    prow_ref[2:3, :] = depth * scale
    for line in range(lines):
        dy = ((me * lines + line).astype(F32) + 0.5) * pixel_step - patch_y
        prow_ref[3 + 2 * line : 4 + 2 * line, :] = dy * scale
        prow_ref[4 + 2 * line : 5 + 2 * line, :] = dy * dy / depth + depth
    pcol_ref[...] = jnp.concatenate([los_ref[...], jnp.zeros((5, npix), F32)], 0).T

    rows = parts * n * ifg_dev
    nifg = n * ifg_dev
    ep = lax.broadcasted_iota(jnp.int32, (NEP, nifg), 0)
    later = (ep == pairs_ref[1:2, :]).astype(F32)
    earlier = (ep == pairs_ref[0:1, :]).astype(F32)
    design = (later - earlier).astype(BF16)
    slot = lax.broadcasted_iota(jnp.int32, (nifg, rows), 1)
    source = slot // (parts * ifg_dev) * ifg_dev + slot % ifg_dev
    spread = (lax.broadcasted_iota(jnp.int32, (nifg, rows), 0) == source).astype(F32).astype(BF16)
    design_half = jnp.dot(design, spread, preferred_element_type=F32).astype(BF16)
    sub = lax.broadcasted_iota(jnp.int32, (NEP, NEP), 0)
    lane = lax.broadcasted_iota(jnp.int32, (NEP, NEP), 1)
    normal = lax.dot_general(design, design, NT, preferred_element_type=F32)
    mat[...] = normal + jnp.where(sub == lane, damping, 0.0)

    def sweep(k):
        m = mat[...]
        col = jnp.sum(jnp.where(lane == k, m, 0.0), axis=1, keepdims=True)
        row = jnp.sum(jnp.where(sub == k, m, 0.0), axis=0, keepdims=True)
        pivot = jnp.sum(jnp.where(lane[0:1] == k, row, 0.0), axis=1, keepdims=True)
        inv = 1.0 / pivot
        scaled = row * inv
        new = m - col * scaled
        new = jnp.where(lane == k, col * inv, new)
        new = jnp.where(sub == k, scaled, new)
        mat[...] = jnp.where((sub == k) & (lane == k), -inv, new)

    strip, wide = 32, 256
    per_line = IMG_W // strip

    for line in range(lines):

        @pl.loop(0, per_line)
        def _(t):
            start = pl.multiple_of(line * IMG_W + t * strip, strip)
            col = pcol_ref[pl.ds(start, strip), :]
            cell = t * strip + lax.broadcasted_iota(jnp.int32, (strip, LANES), 0)
            xpos = (cell.astype(F32) + 0.5) * pixel_step
            east = jnp.broadcast_to(col[:, 0:1], (strip, LANES))
            north = jnp.broadcast_to(col[:, 1:2], (strip, LANES))
            upward = jnp.broadcast_to(col[:, 2:3], (strip, LANES))
            if (line + 1) * per_line <= NEP:
                sweep(line * per_line + t)
            total = jnp.zeros((strip, LANES), F32)
            for c in range(npatch // wide):
                halves = []
                for j in range(wide // LANES):
                    at = slice(c * wide + j * LANES, c * wide + (j + 1) * LANES)
                    u = (xpos - prow_ref[0:1, at]) * prow_ref[1:2, at]
                    r2 = u * u + prow_ref[4 + 2 * line : 5 + 2 * line, at]
                    inv = lax.rsqrt(r2)
                    num = east * u + north * prow_ref[3 + 2 * line : 4 + 2 * line, at]
                    num = num + upward * prow_ref[2:3, at]
                    g = num * (inv * inv * inv)
                    total = total + jnp.abs(g)
                    halves.append(g.astype(BF16))
                green[pl.ds(start, strip), c * wide : (c + 1) * wide] = jnp.concatenate(halves, 1)
            wacc[pl.ds(start, strip), :] = total

    weight = lax.dot_general(
        jnp.ones((EXTRA, LANES), F32),
        wacc[...],
        NT,
        precision=lax.Precision.HIGHEST,
        preferred_element_type=F32,
    ).astype(BF16)
    block = 512

    @pl.loop(0, npatch // block)
    def _(b):
        cols = pl.ds(pl.multiple_of(b * block, block), block)
        row = jnp.dot(weight, jnp.abs(green[:, cols]), preferred_element_type=F32)
        high = row.astype(BF16)
        low = (row - high.astype(F32)).astype(BF16)
        pick = lax.broadcasted_iota(jnp.int32, (EXTRA, block), 0) == 0
        tail = jnp.where(pick, high.astype(F32), low.astype(F32)).astype(BF16)
        for j in range(block // LANES):
            bsend[b * (block // LANES) + j, :, :] = tail[:, j * LANES : (j + 1) * LANES]

    @pl.loop(1, n)
    def _(k):
        d = (me + k) % n
        pltpu.make_async_remote_copy(
            src_ref=bsend.at[d // reps],
            dst_ref=bpart.at[me],
            send_sem=s_b,
            recv_sem=r_b,
            device_id=ident(d),
            device_id_type=mesh_id,
        ).start()

    bpart[me, :, :] = bsend[mine, :, :]

    @pl.loop(min(lines, NEP // per_line) * per_line, NEP)
    def _(k):
        sweep(k)

    inverse = -mat[...]
    inv_hi = inverse.astype(BF16)
    rest = inverse - inv_hi.astype(F32)
    inv_mid = rest.astype(BF16)
    inv_lo = (rest - inv_mid.astype(F32)).astype(BF16)
    pseudo = (
        jnp.dot(inv_hi, design_half, preferred_element_type=F32)
        + jnp.dot(inv_mid, design_half, preferred_element_type=F32)
        + jnp.dot(inv_lo, design_half, preferred_element_type=F32)
    )
    which = (lax.broadcasted_iota(jnp.int32, (NEP, rows), 1) // ifg_dev) % parts

    if chunks == 1:
        own_copy.wait()
    width = npix // parts if chunks == 1 else span
    pieces = []
    for h in range(parts):
        keep = jnp.where(which == h, pseudo, 0.0)
        hi = keep.astype(BF16)
        pieces.append((hi, (keep - hi.astype(F32)).astype(BF16)))

    def solve(c):
        settle(got.at[c], n - 1, r_x.at[c])
        stacked = got[c].reshape(rows, width)
        for h, (hi, lo) in enumerate(pieces):
            piece = jnp.dot(hi, stacked, preferred_element_type=F32)
            piece = piece + jnp.dot(lo, stacked, preferred_element_type=F32)
            at = (c + h) * width
            series[:, at : at + width] = piece
            resid[:, at : at + width] = piece.astype(BF16)

    per_block = block // LANES
    blocks = npatch // block
    first_block = mine // per_block
    side = blocks // 2

    def place(b):
        return (first_block // side + 1 + b // side) % 2 * side + (first_block + 1 + b) % side

    for c in range(chunks - 1):
        solve(c)
        ks = slice(c * span, (c + 1) * span)

        @pl.loop(0, npatch // 1024)
        def _(b):
            cols = pl.ds(pl.multiple_of(b * 1024, 1024), 1024)
            out = jnp.dot(resid[:, ks], green[ks, cols], preferred_element_type=F32)
            if c > 0:
                out = out + guess[:, cols]
            guess[:, cols] = out

    solve(chunks - 1)

    def product(at, first):
        cols = pl.ds(pl.multiple_of(at * block, block), block)
        if first and chunks > 1:
            ks = slice((chunks - 1) * span, npix)
            out = jnp.dot(resid[:, ks], green[ks, cols], preferred_element_type=F32)
            return out + guess[:, cols]
        return jnp.dot(resid[...], green[:, cols], preferred_element_type=F32)

    def bounds():
        settle(bpart, n - 1, r_b)
        settle(bpart, n - 1, s_b)
        both = lax.fori_loop(
            1, n, lambda d, acc: acc + bpart[d].astype(F32), bpart[0].astype(F32)
        )
        return both[0:1] + both[1:2]

    def project(part, recv_sem, pair, pair_sem, first):
        @pl.loop(0, blocks)
        def _(b):
            at = place(b)
            half_out = product(at, first).astype(BF16)
            for j in range(per_block):
                send[at * per_block + j, :, :] = half_out[:, j * LANES : (j + 1) * LANES]
            for j in range(per_block):
                group = at * per_block + j
                for r in range(reps):
                    d = group * reps + r

                    @pl.when(d != me)
                    def _():
                        pltpu.make_async_remote_copy(
                            src_ref=send.at[group],
                            dst_ref=part.at[me],
                            send_sem=s_p,
                            recv_sem=recv_sem,
                            device_id=ident(d),
                            device_id_type=mesh_id,
                        ).start()

        part[me, :, :] = send[mine, :, :]
        settle(part, n - 1, recv_sem)
        settle(part, n - 1, s_p)
        bound = bounds() if first else None
        total = lax.fori_loop(
            1, n, lambda d, acc: acc + part[d].astype(F32), part[0].astype(F32)
        )
        return total, bound

    chips = n // 2
    per_pair = per_block // 2

    def project_split(part, recv_sem, pair, pair_sem, first):
        def forward(at):
            here = pl.ds(at * per_pair, per_pair)
            pltpu.make_async_copy(pair.at[here], pair.at[here], pair_sem.at[at]).wait()
            for j in range(per_pair):
                slot = at * per_pair + j
                send[slot, :, :] = (own[slot] + pair[slot].astype(F32)).astype(BF16)
            for j in range(per_pair):
                slot = at * per_pair + j

                @pl.when(slot != chip)
                def _():
                    pltpu.make_async_remote_copy(
                        src_ref=send.at[slot],
                        dst_ref=part.at[chip],
                        send_sem=s_p,
                        recv_sem=recv_sem,
                        device_id=ident(slot * 2 + core),
                        device_id_type=mesh_id,
                    ).start()

        @pl.loop(0, blocks)
        def _(b):
            at = place(b)
            out = product(at, first)
            for j in range(per_pair):
                even = out[:, 2 * j * LANES : (2 * j + 1) * LANES]
                odd = out[:, (2 * j + 1) * LANES : (2 * j + 2) * LANES]
                slot = at * per_pair + j
                own[slot, :, :] = jnp.where(core == 0, even, odd)
                half[slot, :, :] = jnp.where(core == 0, odd, even).astype(BF16)
            here = pl.ds(at * per_pair, per_pair)
            pltpu.make_async_remote_copy(
                src_ref=half.at[here],
                dst_ref=pair.at[here],
                send_sem=s_h,
                recv_sem=pair_sem.at[at],
                device_id=ident(partner),
                device_id_type=mesh_id,
            ).start()

            @pl.when(b > 0)
            def _():
                forward(place(b - 1))

        forward(place(blocks - 1))
        part[chip, :, :] = send[chip, :, :]
        settle(half, chips, s_h)
        bound = bounds() if first else None
        settle(part, chips - 1, recv_sem)
        settle(part, chips - 1, s_p)
        total = lax.fori_loop(
            1, chips, lambda d, acc: acc + part[d].astype(F32), part[0].astype(F32)
        )
        return total, bound

    tile = 512

    def share(slip, gath, recv_sem, pass_sem, target):
        gath[mine, :, :] = slip.astype(BF16)

        @pl.loop(1, gathered)
        def _(k):
            d = (me + (n - k * reps)) % n
            pltpu.make_async_remote_copy(
                src_ref=gath.at[mine],
                dst_ref=gath.at[mine],
                send_sem=s_g,
                recv_sem=recv_sem.at[first_block],
                device_id=ident(d),
                device_id_type=mesh_id,
            ).start()

        for i in range(blocks):
            at = (first_block + i) % blocks
            settle(gath, per_block - 1 if i == 0 else per_block, recv_sem.at[at])
            for j in range(per_block):
                full[:, j * LANES : (j + 1) * LANES] = gath[at * per_block + j]
            cols = pl.ds(pl.multiple_of(at * block, block), block)

            @pl.loop(0, npix // tile)
            def _(t):
                here = pl.ds(pl.multiple_of(t * tile, tile), tile)
                out = lax.dot_general(
                    full[:, 0:block], green[here, cols], NT, preferred_element_type=F32
                )
                if i > 0:
                    out = target[:, here] + out
                target[:, here] = out

        settle(gath, gathered - 1, s_g)

    def share_split(slip, gath, recv_sem, pass_sem, target):
        mine_at = core * chips + chip
        gath[mine_at, :, :] = slip.astype(BF16)
        each = chips // batches
        home = chip // each

        @pl.loop(1, chips)
        def _(k):
            to = (chip + k) % chips
            pltpu.make_async_remote_copy(
                src_ref=gath.at[mine_at],
                dst_ref=gath.at[mine_at],
                send_sem=s_g,
                recv_sem=recv_sem.at[home],
                device_id=ident(to * 2 + core),
                device_id_type=mesh_id,
            ).start()

        def order(i):
            if batches != 4:
                return (home + i) % batches
            return (home, home + 1 - 2 * (home % 2), (home + 2) % 4, 3 - home)[i]

        def passing(at):
            return pl.ds(core * chips + at * each, each)

        def collect(i):
            at = order(i)
            settle(gath, each - 1 if i == 0 else each, recv_sem.at[at])
            pltpu.make_async_remote_copy(
                src_ref=gath.at[passing(at)],
                dst_ref=gath.at[passing(at)],
                send_sem=s_f,
                recv_sem=pass_sem.at[at],
                device_id=ident(partner),
                device_id_type=mesh_id,
            ).start()

        step = 2 if batches % 2 == 0 else 1
        for i in range(0, batches, step):
            for m in range(step):
                collect(i + m)
            greens = []
            for m in range(step):
                at = order(i + m)
                settle(gath, each, pass_sem.at[at])
                for j in range(each):
                    for p in range(2):
                        lane = (m * 2 * each + 2 * j + p) * LANES
                        full[:, lane : lane + LANES] = gath[p * chips + at * each + j]
                span_at = 2 * each * LANES
                greens.append(pl.ds(pl.multiple_of(at * span_at, span_at), span_at))

            @pl.loop(0, npix // 1024)
            def _(t):
                here = pl.ds(pl.multiple_of(t * 1024, 1024), 1024)
                out = None
                for m in range(step):
                    left = full[:, m * span_at : (m + 1) * span_at]
                    term = lax.dot_general(
                        left, green[here, greens[m]], NT, preferred_element_type=F32
                    )
                    out = term if out is None else out + term
                if i > 0:
                    out = target[:, here] + out
                target[:, here] = out

        settle(gath, chips - 1, s_g)
        settle(gath, chips, s_f)

    if split:
        project, share = project_split, share_split
    sums, bound = project(part_a, r_pa, pair_a, r_ha, True)
    settle(got.at[0], n - 1, s_x)
    for c in range(1, chunks):
        settle(got.at[c], n - 1, s_x)
    slip = sums / bound
    share(slip, gath_a, r_ga, r_fa, guess)
    resid[...] = (series[...] - guess[:, 0:npix]).astype(BF16)
    slip = slip + project(part_b, r_pb, pair_b, r_hb, False)[0] / bound
    slip_ref[...] = slip
    share(slip, gath_b, r_gb, r_fb, pred_ref)


def on_device(interferograms, epoch_pairs, los, patch_place, patch_depth):
    n = lax.axis_size(("pix", "rep"))
    me = lax.axis_index(("pix", "rep"))
    ifg_dev, total = interferograms.shape
    npix = total // n
    npatch = patch_depth.shape[0]
    own = npatch // n
    reps = max(LANES // own, 1)
    parts = max(16 // ifg_dev, 1)
    width = npix // parts
    lines = npix // IMG_W

    chunks = 1
    if ifg_dev % 8 == 0 and lines > 1:
        chunks, parts, width = lines, 1, IMG_W
        xs = interferograms
    else:
        xs = interferograms.astype(BF16).reshape(ifg_dev, n, parts, width)
        xs = xs.transpose(1, 2, 0, 3).reshape(n, parts * ifg_dev, width)
    inside = chunks > 1
    groups = npatch // LANES
    cfg = (n, reps, npix, npatch, parts, ifg_dev, lines, chunks)
    chips = n // 2
    pairs = chips if reps == 1 else 1
    small = (1,) + (16, LANES)
    loads = 8 if n % 8 == 0 else 1
    batches = max(n // 8, 1)
    vmem = pl.BlockSpec(memory_space=pltpu.VMEM)
    piece = (NEP, LANES)
    block = 512
    dma = pltpu.SemaphoreType.DMA
    predicted, slip = pl.pallas_call(
        functools.partial(kernel, cfg),
        out_shape=(
            jax.ShapeDtypeStruct((NEP, npix), F32),
            jax.ShapeDtypeStruct((NEP, LANES), F32),
        ),
        in_specs=[vmem, vmem, vmem, vmem, pl.BlockSpec(memory_space=pl.ANY)],
        out_specs=(vmem, vmem),
        scratch_shapes=[
            pltpu.VMEM((npix, 8), F32),
            pltpu.VMEM((3 + 2 * lines, npatch), F32),
            pltpu.VMEM((NEP, NEP), F32),
            pltpu.VMEM((npix, npatch), BF16),
            pltpu.VMEM((npix, LANES), F32),
            pltpu.VMEM((chunks, n, parts * ifg_dev, width), BF16),
            pltpu.VMEM((NEP, npix), F32),
            pltpu.VMEM((NEP, npix), BF16),
            pltpu.VMEM((groups, EXTRA, LANES), BF16),
            pltpu.VMEM((n, EXTRA, LANES), BF16),
            pltpu.VMEM((groups,) + piece, BF16),
            pltpu.VMEM((n,) + piece, BF16),
            pltpu.VMEM((n,) + piece, BF16),
            pltpu.VMEM((groups, NEP, LANES), BF16),
            pltpu.VMEM((groups, NEP, LANES), BF16),
            pltpu.VMEM((NEP, npatch // 2), BF16),
            pltpu.VMEM((NEP, max(npix, npatch)), F32),
            pltpu.VMEM(interferograms.shape if inside else (8, LANES), F32),
            pltpu.VMEM((chunks, n, ifg_dev, width) if inside else small, BF16),
            pltpu.VMEM((pairs,) + piece, F32),
            pltpu.VMEM((pairs,) + piece, BF16),
            pltpu.VMEM((pairs,) + piece, BF16),
            pltpu.VMEM((pairs,) + piece, BF16),
            dma,
            dma((chunks,)),
            dma((loads,)),
            dma,
            dma,
            dma,
            dma,
            dma,
            dma,
            dma((npatch // block,)),
            dma((npatch // block,)),
            dma,
            dma((max(npatch // block, batches),)),
            dma((max(npatch // block, batches),)),
            dma,
            dma((batches,)),
            dma((batches,)),
        ],
        compiler_params=pltpu.CompilerParams(
            collective_id=0, has_side_effects=True, vmem_limit_bytes=62 * 1024 * 1024
        ),
    )(epoch_pairs, los, patch_place, patch_depth[None], xs)
    if reps > 1:
        slip = lax.dynamic_slice_in_dim(slip, (me % reps) * own, own, 1)
    return (predicted, slip)


def solution(mesh):
    placed = (P(("pix", "rep"), None), P(), P(None, ("pix", "rep")), P(), P())
    return jax.shard_map(
        on_device,
        mesh=mesh,
        in_specs=placed,
        out_specs=(P(None, ("pix", "rep")), P(None, ("pix", "rep"))),
        check_vma=False,
    )
```

profile of v0, /device:TPU:0, one launch (start us, length us, event | category | flops | bytes accessed | tf_op | source)
XLA Modules:
  0.0 126.1 jit_solution(4663770029444507532)
XLA Ops:
  0.6 121.8 %shard_map.68 = (f32[64,4096]{1,0:T(8,128)}, f32[64,128]{1,0:T(8,128)}) custom-call(s32[2,256]{1,0:T(2,128)} %pairs_ref.1, f32[3,4096]{1,0:T(4,128)} %los_ref.1, s32[2,4096]{1,0:T(2,128)} %place_ref.1, s32[1,4096]{1,0:T(1,128)} %bitcast.1, f32[8,131072]{1,0:T(8,128)} %xs_ref.1), custom_call_target="tpu_custom_call" | custom-call | tf_op jit(solution)/shard_map/pallas_call | solution.py:573
  122.4 2.3 %copy.9 = f32[64,4096]{1,0:T(8,128)} copy(f32[64,4096]{1,0:T(8,128)} %get-tuple-element.4) | data formatting | bytes 2097152
  124.7 1.4 %copy.10 = f32[64,128]{1,0:T(8,128)} copy(f32[64,128]{1,0:T(8,128)} %get-tuple-element.5) | data formatting | bytes 65536
where the time goes:
time: 127 us; the launch traced here: 126 us
  Pallas kernels  122 us (96%)
  local copies, waits for them, and re-layouts  3.64 us (3%)
    pallas_call x1, Pallas kernels, on_device(): pl.pallas_call(functools.partial(kernel, cfg), out_shape=(jax.ShapeDtypeS...  122 us
    unnamed x2, local copies, waits for them, and re-layouts  3.64 us

commit v1 on v0

--- a/solution.py
+++ b/solution.py
@@ -11,16 +11,19 @@
 IMG_W = 1024
 LANES = 128
 
-pixel_step = 0.1
-patch_step = 0.4
 damping = 0.5
-depth_base = 0.5
-depth_step = 0.25
 
 F32 = jnp.float32
 BF16 = jnp.bfloat16
 NT = (((1,), (1,)), ((), ()))
 EXTRA = 16
+
+
+def thirds(x):
+    high = x.astype(BF16).astype(F32)
+    rest = x - high
+    mid = rest.astype(BF16).astype(F32)
+    return high, mid, (rest - mid).astype(BF16).astype(F32)
 
 
 def kernel(
@@ -32,8 +35,9 @@
     xs_ref,
     pred_ref,
     slip_ref,
-    pcol_ref,
-    prow_ref,
+    feat,
+    basis,
+    prow,
     mat,
     green,
     wacc,
@@ -126,6 +130,35 @@
                     at = pl.ds(pl.multiple_of(d * npix + c * span, span), span)
                     xsend[c, d, :, :] = stage[:, at].astype(BF16)
 
+    pixel = lax.broadcasted_iota(jnp.int32, (1, npix), 1)
+    odd_x = (2 * (pixel % IMG_W) + 1).astype(F32)
+    odd_y = (2 * (me * lines + pixel // IMG_W) + 1).astype(F32)
+    cell_x = (8 * place_ref[0:1, :] + 4).astype(F32)
+    cell_y = (8 * place_ref[1:2, :] + 4).astype(F32)
+    deep = (10 + 5 * depth_ref[...]).astype(F32)
+    gain = 20.0 * deep
+    left, right = [], []
+    for one, values in (
+        (los_ref[0:1, :] * odd_x, (gain,)),
+        (los_ref[1:2, :] * odd_y, (gain,)),
+        (los_ref[0:1, :], thirds(-gain * cell_x)),
+        (los_ref[1:2, :], thirds(-gain * cell_y)),
+        (los_ref[2:3, :], thirds(gain * deep)[:2]),
+    ):
+        for a in thirds(one):
+            for b in values:
+                left.append(a)
+                right.append(b)
+    spare = feat.shape[1] - len(left)
+    left.append(jnp.zeros((spare, npix), F32))
+    right.append(jnp.zeros((spare, npatch), F32))
+    feat[...] = jnp.concatenate(left, 0).T.astype(BF16)
+    basis[...] = jnp.concatenate(right, 0).astype(BF16)
+    prow[0:1, :] = cell_x
+    for line in range(lines):
+        away = (2 * (me * lines + line) + 1).astype(F32) - cell_y
+        prow[1 + line : 2 + line, :] = away * away + deep * deep
+
     pl.semaphore_wait(barrier, n - 1)
 
     for c in range(chunks):
@@ -148,19 +181,6 @@
     else:
         own_copy = pltpu.make_async_copy(xs_ref.at[me], got.at[0, me], r_in.at[0])
         own_copy.start()
-
-    patch_x = (place_ref[0:1, :].astype(F32) + 0.5) * patch_step
-    patch_y = (place_ref[1:2, :].astype(F32) + 0.5) * patch_step
-    depth = depth_base + depth_step * depth_ref[...].astype(F32)
-    scale = lax.rsqrt(depth)
-    prow_ref[0:1, :] = patch_x
-    prow_ref[1:2, :] = scale
-    prow_ref[2:3, :] = depth * scale
-    for line in range(lines):
-        dy = ((me * lines + line).astype(F32) + 0.5) * pixel_step - patch_y
-        prow_ref[3 + 2 * line : 4 + 2 * line, :] = dy * scale
-        prow_ref[4 + 2 * line : 5 + 2 * line, :] = dy * dy / depth + depth
-    pcol_ref[...] = jnp.concatenate([los_ref[...], jnp.zeros((5, npix), F32)], 0).T
 
     rows = parts * n * ifg_dev
     nifg = n * ifg_dev
@@ -181,45 +201,48 @@
         m = mat[...]
         col = jnp.sum(jnp.where(lane == k, m, 0.0), axis=1, keepdims=True)
         row = jnp.sum(jnp.where(sub == k, m, 0.0), axis=0, keepdims=True)
-        pivot = jnp.sum(jnp.where(lane[0:1] == k, row, 0.0), axis=1, keepdims=True)
+        wide_col = jnp.broadcast_to(col, (NEP, NEP))
+        pivot = jnp.sum(jnp.where(sub == k, wide_col, 0.0), axis=0, keepdims=True)
         inv = 1.0 / pivot
         scaled = row * inv
-        new = m - col * scaled
-        new = jnp.where(lane == k, col * inv, new)
+        new = m - wide_col * scaled
+        new = jnp.where(lane == k, wide_col * inv, new)
         new = jnp.where(sub == k, scaled, new)
         mat[...] = jnp.where((sub == k) & (lane == k), -inv, new)
 
-    strip, wide = 32, 256
+    strip, wide = 128, 256
     per_line = IMG_W // strip
-
-    for line in range(lines):
-
+    turns = 2 * -(-NEP // (lines * per_line))
+    swept = min(lines, NEP // (per_line * turns)) * per_line * turns
+
+    def generate(line):
         @pl.loop(0, per_line)
         def _(t):
             start = pl.multiple_of(line * IMG_W + t * strip, strip)
-            col = pcol_ref[pl.ds(start, strip), :]
-            cell = t * strip + lax.broadcasted_iota(jnp.int32, (strip, LANES), 0)
-            xpos = (cell.astype(F32) + 0.5) * pixel_step
-            east = jnp.broadcast_to(col[:, 0:1], (strip, LANES))
-            north = jnp.broadcast_to(col[:, 1:2], (strip, LANES))
-            upward = jnp.broadcast_to(col[:, 2:3], (strip, LANES))
-            if (line + 1) * per_line <= NEP:
-                sweep(line * per_line + t)
+            mix = feat[pl.ds(start, strip), :]
+            spot = t * strip + lax.broadcasted_iota(jnp.int32, (strip, LANES), 0)
+            xpos = (2 * spot + 1).astype(F32)
+            for q in range(turns):
+                if (line + 1) * per_line * turns <= swept:
+                    sweep((line * per_line + t) * turns + q)
             total = jnp.zeros((strip, LANES), F32)
             for c in range(npatch // wide):
+                num = jnp.dot(
+                    mix, basis[:, c * wide : (c + 1) * wide], preferred_element_type=F32
+                )
                 halves = []
                 for j in range(wide // LANES):
                     at = slice(c * wide + j * LANES, c * wide + (j + 1) * LANES)
-                    u = (xpos - prow_ref[0:1, at]) * prow_ref[1:2, at]
-                    r2 = u * u + prow_ref[4 + 2 * line : 5 + 2 * line, at]
-                    inv = lax.rsqrt(r2)
-                    num = east * u + north * prow_ref[3 + 2 * line : 4 + 2 * line, at]
-                    num = num + upward * prow_ref[2:3, at]
-                    g = num * (inv * inv * inv)
+                    away = xpos - prow[0:1, at]
+                    inv = lax.rsqrt(away * away + prow[1 + line : 2 + line, at])
+                    g = num[:, j * LANES : (j + 1) * LANES] * (inv * inv * inv)
                     total = total + jnp.abs(g)
                     halves.append(g.astype(BF16))
                 green[pl.ds(start, strip), c * wide : (c + 1) * wide] = jnp.concatenate(halves, 1)
             wacc[pl.ds(start, strip), :] = total
+
+    for line in range(lines):
+        generate(line)
 
     weight = lax.dot_general(
         jnp.ones((EXTRA, LANES), F32),
@@ -255,7 +278,7 @@
 
     bpart[me, :, :] = bsend[mine, :, :]
 
-    @pl.loop(min(lines, NEP // per_line) * per_line, NEP)
+    @pl.loop(swept, NEP)
     def _(k):
         sweep(k)
 
@@ -579,8 +602,9 @@
         in_specs=[vmem, vmem, vmem, vmem, pl.BlockSpec(memory_space=pl.ANY)],
         out_specs=(vmem, vmem),
         scratch_shapes=[
-            pltpu.VMEM((npix, 8), F32),
-            pltpu.VMEM((3 + 2 * lines, npatch), F32),
+            pltpu.VMEM((npix, 32), BF16),
+            pltpu.VMEM((32, npatch), BF16),
+            pltpu.VMEM((1 + lines, npatch), F32),
             pltpu.VMEM((NEP, NEP), F32),
             pltpu.VMEM((npix, npatch), BF16),
             pltpu.VMEM((npix, LANES), F32),

time: 127 us -> 119 us (0.937)
  Pallas kernels: 122 us -> 115 us
    pallas_call x1, Pallas kernels: 122 us -> 115 us  [on_device(): pl.pallas_call(functools.partial(kernel, cfg), out_shape=(jax.ShapeDtypeS...]
where the time goes in v1:
time: 119 us
  Pallas kernels  115 us (97%)
  local copies, waits for them, and re-layouts  3.64 us (3%)
    pallas_call x1, Pallas kernels, on_device(): pl.pallas_call(functools.partial(kernel, cfg), out_shape=(jax.ShapeDtypeS...  115 us
    unnamed x2, local copies, waits for them, and re-layouts  3.64 us

profile of v1, /device:TPU:0, one launch (start us, length us, event | category | flops | bytes accessed | tf_op | source)
XLA Modules:
  0.0 119.1 jit_solution(15798904356409991029)
XLA Ops:
  0.6 114.8 %shard_map.68 = (f32[64,4096]{1,0:T(8,128)}, f32[64,128]{1,0:T(8,128)}) custom-call(s32[2,256]{1,0:T(2,128)} %pairs_ref.1, f32[3,4096]{1,0:T(4,128)} %los_ref.1, s32[2,4096]{1,0:T(2,128)} %place_ref.1, s32[1,4096]{1,0:T(1,128)} %bitcast.1, f32[8,131072]{1,0:T(8,128)} %xs_ref.1), custom_call_target="tpu_custom_call" | custom-call | tf_op jit(solution)/shard_map/pallas_call | solution.py:596
  115.5 2.3 %copy.9 = f32[64,4096]{1,0:T(8,128)} copy(f32[64,4096]{1,0:T(8,128)} %get-tuple-element.4) | data formatting | bytes 2097152
  117.7 1.4 %copy.10 = f32[64,128]{1,0:T(8,128)} copy(f32[64,128]{1,0:T(8,128)} %get-tuple-element.5) | data formatting | bytes 65536

commit v2 on v1

--- a/solution.py
+++ b/solution.py
@@ -41,6 +41,8 @@
     mat,
     green,
     wacc,
+    weight,
+    brow,
     got,
     series,
     resid,
@@ -52,6 +54,7 @@
     gath_a,
     gath_b,
     full,
+    tall,
     guess,
     stage,
     xsend,
@@ -215,9 +218,34 @@
     turns = 2 * -(-NEP // (lines * per_line))
     swept = min(lines, NEP // (per_line * turns)) * per_line * turns
 
+    slab = npatch // per_line
+
+    def weigh(line):
+        here = slice(line * IMG_W, (line + 1) * IMG_W)
+        weight[...] = lax.dot_general(
+            jnp.ones((EXTRA, LANES), F32),
+            wacc[here, :],
+            NT,
+            precision=lax.Precision.HIGHEST,
+            preferred_element_type=F32,
+        ).astype(BF16)
+
+    def gather_bound(line, t):
+        here = slice(line * IMG_W, (line + 1) * IMG_W)
+        cols = pl.ds(pl.multiple_of(t * slab, slab), slab)
+        row = jnp.dot(weight[...], jnp.abs(green[here, cols]), preferred_element_type=F32)
+        if line > 0:
+            row = row + brow[:, cols]
+        brow[:, cols] = row
+
     def generate(line):
+        if line > 0:
+            weigh(line - 1)
+
         @pl.loop(0, per_line)
         def _(t):
+            if line > 0:
+                gather_bound(line - 1, t)
             start = pl.multiple_of(line * IMG_W + t * strip, strip)
             mix = feat[pl.ds(start, strip), :]
             spot = t * strip + lax.broadcasted_iota(jnp.int32, (strip, LANES), 0)
@@ -244,25 +272,19 @@
     for line in range(lines):
         generate(line)
 
-    weight = lax.dot_general(
-        jnp.ones((EXTRA, LANES), F32),
-        wacc[...],
-        NT,
-        precision=lax.Precision.HIGHEST,
-        preferred_element_type=F32,
-    ).astype(BF16)
     block = 512
-
-    @pl.loop(0, npatch // block)
+    weigh(lines - 1)
+
+    @pl.loop(0, npatch // slab)
     def _(b):
-        cols = pl.ds(pl.multiple_of(b * block, block), block)
-        row = jnp.dot(weight, jnp.abs(green[:, cols]), preferred_element_type=F32)
+        gather_bound(lines - 1, b)
+        row = brow[:, pl.ds(pl.multiple_of(b * slab, slab), slab)]
         high = row.astype(BF16)
         low = (row - high.astype(F32)).astype(BF16)
-        pick = lax.broadcasted_iota(jnp.int32, (EXTRA, block), 0) == 0
+        pick = lax.broadcasted_iota(jnp.int32, (EXTRA, slab), 0) == 0
         tail = jnp.where(pick, high.astype(F32), low.astype(F32)).astype(BF16)
-        for j in range(block // LANES):
-            bsend[b * (block // LANES) + j, :, :] = tail[:, j * LANES : (j + 1) * LANES]
+        for j in range(slab // LANES):
+            bsend[b * (slab // LANES) + j, :, :] = tail[:, j * LANES : (j + 1) * LANES]
 
     @pl.loop(1, n)
     def _(k):
@@ -478,35 +500,50 @@
 
         settle(gath, gathered - 1, s_g)
 
+    each = chips // batches
+    home = chip // each
+    span_at = 2 * each * LANES
+
     def share_split(slip, gath, recv_sem, pass_sem, target):
         mine_at = core * chips + chip
         gath[mine_at, :, :] = slip.astype(BF16)
-        each = chips // batches
-        home = chip // each
-
-        @pl.loop(1, chips)
-        def _(k):
-            to = (chip + k) % chips
+
+        def give(to, side_core):
             pltpu.make_async_remote_copy(
                 src_ref=gath.at[mine_at],
                 dst_ref=gath.at[mine_at],
                 send_sem=s_g,
                 recv_sem=recv_sem.at[home],
-                device_id=ident(to * 2 + core),
+                device_id=ident(to * 2 + side_core),
                 device_id_type=mesh_id,
             ).start()
+
+        give(chip, 1 - core)
+        for k in range(1, each):
+            to = home * each + (chip + k) % each
+            give(to, core)
+            give(to, 1 - core)
 
         def order(i):
             if batches != 4:
                 return (home + i) % batches
-            return (home, home + 1 - 2 * (home % 2), (home + 2) % 4, 3 - home)[i]
+            low, high = i % 2, i // 2
+            bit = home % 2
+            near = bit + low - 2 * bit * low
+            far = home // 2 + high - 2 * (home // 2) * high
+            return 2 * far + near
+
+        @pl.loop(1, batches)
+        def _(i):
+            for k in range(each):
+                give(order(i) * each + (chip + k) % each, core)
 
         def passing(at):
             return pl.ds(core * chips + at * each, each)
 
         def collect(i):
             at = order(i)
-            settle(gath, each - 1 if i == 0 else each, recv_sem.at[at])
+            settle(gath, each, recv_sem.at[at])
             pltpu.make_async_remote_copy(
                 src_ref=gath.at[passing(at)],
                 dst_ref=gath.at[passing(at)],
@@ -516,37 +553,53 @@
                 device_id_type=mesh_id,
             ).start()
 
-        step = 2 if batches % 2 == 0 else 1
-        for i in range(0, batches, step):
-            for m in range(step):
-                collect(i + m)
-            greens = []
-            for m in range(step):
-                at = order(i + m)
+        target[:, 0:npix] = jnp.zeros((NEP, npix), F32)
+        groups_in = 4
+        rounds = npix // (1024 * groups_in)
+
+        @pl.loop(0, batches)
+        def _(i):
+            at = order(i)
+
+            @pl.when(i == 0)
+            def _():
+                settle(gath, 2 * each - 1, recv_sem.at[at])
+
+            @pl.when(i > 0)
+            def _():
                 settle(gath, each, pass_sem.at[at])
-                for j in range(each):
-                    for p in range(2):
-                        lane = (m * 2 * each + 2 * j + p) * LANES
-                        full[:, lane : lane + LANES] = gath[p * chips + at * each + j]
-                span_at = 2 * each * LANES
-                greens.append(pl.ds(pl.multiple_of(at * span_at, span_at), span_at))
-
-            @pl.loop(0, npix // 1024)
-            def _(t):
-                here = pl.ds(pl.multiple_of(t * 1024, 1024), 1024)
-                out = None
-                for m in range(step):
-                    left = full[:, m * span_at : (m + 1) * span_at]
-                    term = lax.dot_general(
-                        left, green[here, greens[m]], NT, preferred_element_type=F32
-                    )
-                    out = term if out is None else out + term
-                if i > 0:
-                    out = target[:, here] + out
-                target[:, here] = out
-
-        settle(gath, chips - 1, s_g)
-        settle(gath, chips, s_f)
+
+            for j in range(each):
+                for p in range(2):
+                    lane = (2 * j + p) * LANES
+                    full[:, lane : lane + LANES] = gath[p * chips + at * each + j]
+            tall[...] = full[:, 0:span_at].T
+
+            @pl.loop(0, rounds)
+            def _(trip):
+                @pl.when((i + 1 < batches) & (trip == rounds // 2))
+                def _():
+                    collect(i + 1)
+
+                for sub_trip in range(groups_in):
+                    start = (trip * groups_in + sub_trip) * 1024
+                    flat = pl.ds(pl.multiple_of(start, 512), 512)
+                    long = pl.ds(pl.multiple_of(start + 512, 512), 512)
+                    wide_out = long_out = None
+                    for k in range(0, span_at, 256):
+                        ks = slice(k, k + 256)
+                        cols = pl.ds(pl.multiple_of(at * span_at + k, 256), 256)
+                        a = lax.dot_general(
+                            full[:, ks], green[flat, cols], NT, preferred_element_type=F32
+                        )
+                        b = jnp.dot(green[long, cols], tall[ks, :], preferred_element_type=F32)
+                        wide_out = a if wide_out is None else wide_out + a
+                        long_out = b if long_out is None else long_out + b
+                    target[:, flat] = target[:, flat] + wide_out
+                    target[:, long] = target[:, long] + long_out.T
+
+        settle(gath, 2 * each - 1 + (batches - 1) * each, s_g)
+        settle(gath, (batches - 1) * each, s_f)
 
     if split:
         project, share = project_split, share_split
@@ -560,6 +613,24 @@
     slip = slip + project(part_b, r_pb, pair_b, r_hb, False)[0] / bound
     slip_ref[...] = slip
     share(slip, gath_b, r_gb, r_fb, pred_ref)
+
+
+def relay(pred_ref, slip_ref, pred_out, slip_out, pred_buf, slip_buf, sems):
+    rows = 8
+    count = pred_ref.shape[0] // rows
+    moves = [(slip_ref, slip_buf, slip_out)]
+    for i in range(count):
+        at = pl.ds(i * rows, rows)
+        moves.append((pred_ref.at[at], pred_buf.at[at], pred_out.at[at]))
+    loads = [pltpu.make_async_copy(a, b, sems.at[0, i]) for i, (a, b, c) in enumerate(moves)]
+    stores = [pltpu.make_async_copy(b, c, sems.at[1, i]) for i, (a, b, c) in enumerate(moves)]
+    for load in loads:
+        load.start()
+    for load, store in zip(loads, stores):
+        load.wait()
+        store.start()
+    for store in stores:
+        store.wait()
 
 
 def on_device(interferograms, epoch_pairs, los, patch_place, patch_depth):
@@ -608,6 +679,8 @@
             pltpu.VMEM((NEP, NEP), F32),
             pltpu.VMEM((npix, npatch), BF16),
             pltpu.VMEM((npix, LANES), F32),
+            pltpu.VMEM((EXTRA, IMG_W), BF16),
+            pltpu.VMEM((EXTRA, npatch), F32),
             pltpu.VMEM((chunks, n, parts * ifg_dev, width), BF16),
             pltpu.VMEM((NEP, npix), F32),
             pltpu.VMEM((NEP, npix), BF16),
@@ -618,7 +691,8 @@
             pltpu.VMEM((n,) + piece, BF16),
             pltpu.VMEM((groups, NEP, LANES), BF16),
             pltpu.VMEM((groups, NEP, LANES), BF16),
-            pltpu.VMEM((NEP, npatch // 2), BF16),
+            pltpu.VMEM((NEP, max(block, 2 * LANES * chips // batches)), BF16),
+            pltpu.VMEM((2 * LANES * chips // batches, NEP), BF16),
             pltpu.VMEM((NEP, max(npix, npatch)), F32),
             pltpu.VMEM(interferograms.shape if inside else (8, LANES), F32),
             pltpu.VMEM((chunks, n, ifg_dev, width) if inside else small, BF16),
@@ -648,6 +722,18 @@
             collective_id=0, has_side_effects=True, vmem_limit_bytes=62 * 1024 * 1024
         ),
     )(epoch_pairs, los, patch_place, patch_depth[None], xs)
+    anywhere = pl.BlockSpec(memory_space=pl.ANY)
+    predicted, slip = pl.pallas_call(
+        relay,
+        out_shape=tuple(jax.ShapeDtypeStruct(a.shape, F32) for a in (predicted, slip)),
+        in_specs=[anywhere, anywhere],
+        out_specs=(anywhere, anywhere),
+        scratch_shapes=[
+            pltpu.VMEM(predicted.shape, F32),
+            pltpu.VMEM(slip.shape, F32),
+            dma((2, 1 + NEP // 8)),
+        ],
+    )(predicted, slip)
     if reps > 1:
         slip = lax.dynamic_slice_in_dim(slip, (me % reps) * own, own, 1)
     return (predicted, slip)

time: 119 us -> 111 us (0.933)
  Pallas kernels: 115 us -> 110 us
  local copies, waits for them, and re-layouts: 3.64 us -> 0 us
    pallas_call x1, Pallas kernels: 115 us -> 108 us  [on_device(): pl.pallas_call(functools.partial(kernel, cfg), out_shape=(jax.ShapeDtypeS...]
    unnamed x2 -> x0, local copies, waits for them, and re-layouts: 3.64 us -> none
    pallas_call x0 -> x1, Pallas kernels: none -> 2.12 us  [on_device(): pl.pallas_call(relay, out_shape=tuple((jax.ShapeDtypeStruct(a.shape, F32)...]
where the time goes in v2:
time: 111 us
  Pallas kernels  110 us (99%)
    pallas_call x1, Pallas kernels, on_device(): pl.pallas_call(functools.partial(kernel, cfg), out_shape=(jax.ShapeDtypeS...  108 us

profile of v2, /device:TPU:0, one launch (start us, length us, event | category | flops | bytes accessed | tf_op | source)
XLA Modules:
  0.0 110.7 jit_solution(5043599190328105581)
XLA Ops:
  0.6 107.9 %shard_map.68 = (f32[64,4096]{1,0:T(8,128)}, f32[64,128]{1,0:T(8,128)}) custom-call(s32[2,256]{1,0:T(2,128)} %pairs_ref.1, f32[3,4096]{1,0:T(4,128)} %los_ref.1, s32[2,4096]{1,0:T(2,128)} %place_ref.1, s32[1,4096]{1,0:T(1,128)} %bitcast.1, f32[8,131072]{1,0:T(8,128)} %xs_ref.1), custom_call_target="tpu_custom_call" | custom-call | tf_op jit(solution)/shard_map/pallas_call | solution.py:667
  108.6 2.1 %shard_map.69 = (f32[64,4096]{1,0:T(8,128)}, f32[64,128]{1,0:T(8,128)}) custom-call(f32[64,4096]{1,0:T(8,128)} %get-tuple-element.4.pred_ref, f32[64,128]{1,0:T(8,128)} %get-tuple-element.5.slip_ref), custom_call_target="tpu_custom_call" | custom-call | tf_op jit(solution)/shard_map/pallas_call | solution.py:726

commit v3 on v2

--- a/solution.py
+++ b/solution.py
@@ -58,6 +58,8 @@
     guess,
     stage,
     xsend,
+    over,
+    back,
     own,
     half,
     pair_a,
@@ -65,6 +67,8 @@
     s_x,
     r_x,
     r_in,
+    s_m,
+    r_m,
     s_b,
     r_b,
     s_p,
@@ -91,6 +95,10 @@
     chip = me // 2
     partner = me + 1 - 2 * core
     batches = n // 8
+    many = n // 2
+    slot_me = me % many
+    half_me = me // many
+    mirror = (me + many) % n
     mesh_id = pl.DeviceIdType.MESH
 
     def ident(d):
@@ -119,19 +127,6 @@
                 stage.at[:, pl.ds(i * wide_load, wide_load)],
                 r_in.at[i],
             ).start()
-        for i in range(loads):
-            pltpu.make_async_copy(
-                xs_ref.at[:, pl.ds(i * wide_load, wide_load)],
-                stage.at[:, pl.ds(i * wide_load, wide_load)],
-                r_in.at[i],
-            ).wait()
-
-            @pl.loop(0, per_load)
-            def _(j):
-                d = i * per_load + j
-                for c in range(chunks):
-                    at = pl.ds(pl.multiple_of(d * npix + c * span, span), span)
-                    xsend[c, d, :, :] = stage[:, at].astype(BF16)
 
     pixel = lax.broadcasted_iota(jnp.int32, (1, npix), 1)
     odd_x = (2 * (pixel % IMG_W) + 1).astype(F32)
@@ -162,26 +157,55 @@
         away = (2 * (me * lines + line) + 1).astype(F32) - cell_y
         prow[1 + line : 2 + line, :] = away * away + deep * deep
 
+    if chunks > 1:
+        for i in range(loads):
+            pltpu.make_async_copy(
+                xs_ref.at[:, pl.ds(i * wide_load, wide_load)],
+                stage.at[:, pl.ds(i * wide_load, wide_load)],
+                r_in.at[i],
+            ).wait()
+
+            @pl.loop(0, per_load)
+            def _(j):
+                d = i * per_load + j
+                for c in range(chunks):
+                    at = pl.ds(pl.multiple_of(d * npix + c * span, span), span)
+                    side_d = (d // many + half_me) % 2
+                    xsend[c, d % many, side_d, :, :] = stage[:, at].astype(BF16)
+
     pl.semaphore_wait(barrier, n - 1)
 
-    for c in range(chunks):
+    if chunks > 1:
+        for c in range(chunks):
+
+            @pl.loop(1, many)
+            def _(k):
+                to = (slot_me + k) % many
+                pltpu.make_async_remote_copy(
+                    src_ref=xsend.at[c, to],
+                    dst_ref=got.at[c, slot_me],
+                    send_sem=s_x,
+                    recv_sem=r_x.at[c],
+                    device_id=ident(half_me * many + to),
+                    device_id_type=mesh_id,
+                ).start()
+
+        for c in range(chunks):
+            got[c, slot_me, :, :, :] = xsend[c, slot_me, :, :, :]
+    else:
 
         @pl.loop(1, n)
         def _(k):
             d = (me + k) % n
             pltpu.make_async_remote_copy(
-                src_ref=xsend.at[c, d] if chunks > 1 else xs_ref.at[d],
-                dst_ref=got.at[c, me],
+                src_ref=xs_ref.at[d],
+                dst_ref=got.at[0, me],
                 send_sem=s_x,
-                recv_sem=r_x.at[c],
+                recv_sem=r_x.at[0],
                 device_id=ident(d),
                 device_id_type=mesh_id,
             ).start()
 
-    if chunks > 1:
-        for c in range(chunks):
-            got[c, me, :, :] = xsend[c, me, :, :]
-    else:
         own_copy = pltpu.make_async_copy(xs_ref.at[me], got.at[0, me], r_in.at[0])
         own_copy.start()
 
@@ -269,8 +293,63 @@
                 green[pl.ds(start, strip), c * wide : (c + 1) * wide] = jnp.concatenate(halves, 1)
             wacc[pl.ds(start, strip), :] = total
 
+    def invert():
+        @pl.loop(swept, NEP)
+        def _(k):
+            sweep(k)
+
+        inverse = -mat[...]
+        inv_hi = inverse.astype(BF16)
+        rest = inverse - inv_hi.astype(F32)
+        inv_mid = rest.astype(BF16)
+        inv_lo = (rest - inv_mid.astype(F32)).astype(BF16)
+        pseudo = (
+            jnp.dot(inv_hi, design_half, preferred_element_type=F32)
+            + jnp.dot(inv_mid, design_half, preferred_element_type=F32)
+            + jnp.dot(inv_lo, design_half, preferred_element_type=F32)
+        )
+        which = (lax.broadcasted_iota(jnp.int32, (NEP, rows), 1) // ifg_dev) % parts
+        if chunks > 1:
+            cut = many * ifg_dev
+            parted = [jnp.where(half_me == 0, pseudo[:, :cut], pseudo[:, cut:])]
+        else:
+            parted = [jnp.where(which == h, pseudo, 0.0) for h in range(parts)]
+        result = []
+        for keep in parted:
+            hi = keep.astype(BF16)
+            result.append((hi, (keep - hi.astype(F32)).astype(BF16)))
+        return result
+
+    def halve(c):
+        settle(got.at[c], many - 1, r_x.at[c])
+        ((hi, lo),) = pieces
+        sums = []
+        for part_of in range(2):
+            stacked = got[c, :, part_of].reshape(many * ifg_dev, span)
+            piece = jnp.dot(hi, stacked, preferred_element_type=F32)
+            sums.append(piece + jnp.dot(lo, stacked, preferred_element_type=F32))
+        over[c, :, :] = sums[1].astype(BF16)
+        pltpu.make_async_remote_copy(
+            src_ref=over.at[c],
+            dst_ref=back.at[c],
+            send_sem=s_m,
+            recv_sem=r_m.at[c],
+            device_id=ident(mirror),
+            device_id_type=mesh_id,
+        ).start()
+        series[:, c * span : (c + 1) * span] = sums[0]
+
+    ready = min(lines, -(-NEP // (per_line * turns)))
+    halved = 0
     for line in range(lines):
         generate(line)
+        if line == ready - 1:
+            pieces = invert()
+        if chunks > 1 and line >= ready - 1:
+            upto = chunks if line == lines - 1 else min(line + 1, chunks)
+            for c in range(halved, upto):
+                halve(c)
+            halved = upto
 
     block = 512
     weigh(lines - 1)
@@ -300,40 +379,25 @@
 
     bpart[me, :, :] = bsend[mine, :, :]
 
-    @pl.loop(swept, NEP)
-    def _(k):
-        sweep(k)
-
-    inverse = -mat[...]
-    inv_hi = inverse.astype(BF16)
-    rest = inverse - inv_hi.astype(F32)
-    inv_mid = rest.astype(BF16)
-    inv_lo = (rest - inv_mid.astype(F32)).astype(BF16)
-    pseudo = (
-        jnp.dot(inv_hi, design_half, preferred_element_type=F32)
-        + jnp.dot(inv_mid, design_half, preferred_element_type=F32)
-        + jnp.dot(inv_lo, design_half, preferred_element_type=F32)
-    )
-    which = (lax.broadcasted_iota(jnp.int32, (NEP, rows), 1) // ifg_dev) % parts
-
     if chunks == 1:
         own_copy.wait()
-    width = npix // parts if chunks == 1 else span
-    pieces = []
-    for h in range(parts):
-        keep = jnp.where(which == h, pseudo, 0.0)
-        hi = keep.astype(BF16)
-        pieces.append((hi, (keep - hi.astype(F32)).astype(BF16)))
 
     def solve(c):
-        settle(got.at[c], n - 1, r_x.at[c])
-        stacked = got[c].reshape(rows, width)
+        if chunks > 1:
+            here = slice(c * span, (c + 1) * span)
+            pltpu.make_async_copy(back.at[c], back.at[c], r_m.at[c]).wait()
+            piece = series[:, here] + back[c].astype(F32)
+            series[:, here] = piece
+            resid[:, here] = piece.astype(BF16)
+            return
+        settle(got.at[0], n - 1, r_x.at[0])
+        width = npix // parts
+        stacked = got[0].reshape(rows, width)
         for h, (hi, lo) in enumerate(pieces):
             piece = jnp.dot(hi, stacked, preferred_element_type=F32)
             piece = piece + jnp.dot(lo, stacked, preferred_element_type=F32)
-            at = (c + h) * width
-            series[:, at : at + width] = piece
-            resid[:, at : at + width] = piece.astype(BF16)
+            series[:, h * width : (h + 1) * width] = piece
+            resid[:, h * width : (h + 1) * width] = piece.astype(BF16)
 
     per_block = block // LANES
     blocks = npatch // block
@@ -604,9 +668,12 @@
     if split:
         project, share = project_split, share_split
     sums, bound = project(part_a, r_pa, pair_a, r_ha, True)
-    settle(got.at[0], n - 1, s_x)
-    for c in range(1, chunks):
-        settle(got.at[c], n - 1, s_x)
+    if chunks > 1:
+        for c in range(chunks):
+            settle(got.at[c], many - 1, s_x)
+        settle(over, chunks, s_m)
+    else:
+        settle(got.at[0], n - 1, s_x)
     slip = sums / bound
     share(slip, gath_a, r_ga, r_fa, guess)
     resid[...] = (series[...] - guess[:, 0:npix]).astype(BF16)
@@ -653,6 +720,7 @@
         xs = interferograms.astype(BF16).reshape(ifg_dev, n, parts, width)
         xs = xs.transpose(1, 2, 0, 3).reshape(n, parts * ifg_dev, width)
     inside = chunks > 1
+    swap = (chunks, n // 2, 2, ifg_dev, width)
     groups = npatch // LANES
     cfg = (n, reps, npix, npatch, parts, ifg_dev, lines, chunks)
     chips = n // 2
@@ -681,7 +749,7 @@
             pltpu.VMEM((npix, LANES), F32),
             pltpu.VMEM((EXTRA, IMG_W), BF16),
             pltpu.VMEM((EXTRA, npatch), F32),
-            pltpu.VMEM((chunks, n, parts * ifg_dev, width), BF16),
+            pltpu.VMEM(swap if inside else (1, n, parts * ifg_dev, width), BF16),
             pltpu.VMEM((NEP, npix), F32),
             pltpu.VMEM((NEP, npix), BF16),
             pltpu.VMEM((groups, EXTRA, LANES), BF16),
@@ -695,7 +763,9 @@
             pltpu.VMEM((2 * LANES * chips // batches, NEP), BF16),
             pltpu.VMEM((NEP, max(npix, npatch)), F32),
             pltpu.VMEM(interferograms.shape if inside else (8, LANES), F32),
-            pltpu.VMEM((chunks, n, ifg_dev, width) if inside else small, BF16),
+            pltpu.VMEM(swap if inside else small, BF16),
+            pltpu.VMEM((chunks, NEP, width) if inside else small, BF16),
+            pltpu.VMEM((chunks, NEP, width) if inside else small, BF16),
             pltpu.VMEM((pairs,) + piece, F32),
             pltpu.VMEM((pairs,) + piece, BF16),
             pltpu.VMEM((pairs,) + piece, BF16),
@@ -703,6 +773,8 @@
             dma,
             dma((chunks,)),
             dma((loads,)),
+            dma,
+            dma((chunks,)),
             dma,
             dma,
             dma,

time: 111 us -> 105 us (0.946)
  Pallas kernels: 110 us -> 104 us
    pallas_call x1, Pallas kernels: 108 us -> 102 us  [on_device(): pl.pallas_call(functools.partial(kernel, cfg), out_shape=(jax.ShapeDtypeS...]
where the time goes in v3:
time: 105 us
  Pallas kernels  104 us (99%)
    pallas_call x1, Pallas kernels, on_device(): pl.pallas_call(functools.partial(kernel, cfg), out_shape=(jax.ShapeDtypeS...  102 us
    pallas_call x1, Pallas kernels, on_device(): pl.pallas_call(relay, out_shape=tuple((jax.ShapeDtypeStruct(a.shape, F32)...  2.12 us

profile of v3, /device:TPU:0, one launch (start us, length us, event | category | flops | bytes accessed | tf_op | source)
XLA Modules:
  0.0 105.0 jit_solution(16924520345309391612)
XLA Ops:
  0.6 102.3 %shard_map.68 = (f32[64,4096]{1,0:T(8,128)}, f32[64,128]{1,0:T(8,128)}) custom-call(s32[2,256]{1,0:T(2,128)} %pairs_ref.1, f32[3,4096]{1,0:T(4,128)} %los_ref.1, s32[2,4096]{1,0:T(2,128)} %place_ref.1, s32[1,4096]{1,0:T(1,128)} %bitcast.1, f32[8,131072]{1,0:T(8,128)} %xs_ref.1), custom_call_target="tpu_custom_call" | custom-call | tf_op jit(solution)/shard_map/pallas_call | solution.py:735
  102.9 2.1 %shard_map.69 = (f32[64,4096]{1,0:T(8,128)}, f32[64,128]{1,0:T(8,128)}) custom-call(f32[64,4096]{1,0:T(8,128)} %get-tuple-element.4.pred_ref, f32[64,128]{1,0:T(8,128)} %get-tuple-element.5.slip_ref), custom_call_target="tpu_custom_call" | custom-call | tf_op jit(solution)/shard_map/pallas_call | solution.py:798

commit v4 on v3

--- a/solution.py
+++ b/solution.py
@@ -618,8 +618,6 @@
             ).start()
 
         target[:, 0:npix] = jnp.zeros((NEP, npix), F32)
-        groups_in = 4
-        rounds = npix // (1024 * groups_in)
 
         @pl.loop(0, batches)
         def _(i):
@@ -639,28 +637,25 @@
                     full[:, lane : lane + LANES] = gath[p * chips + at * each + j]
             tall[...] = full[:, 0:span_at].T
 
-            @pl.loop(0, rounds)
-            def _(trip):
-                @pl.when((i + 1 < batches) & (trip == rounds // 2))
-                def _():
-                    collect(i + 1)
-
-                for sub_trip in range(groups_in):
-                    start = (trip * groups_in + sub_trip) * 1024
-                    flat = pl.ds(pl.multiple_of(start, 512), 512)
-                    long = pl.ds(pl.multiple_of(start + 512, 512), 512)
-                    wide_out = long_out = None
-                    for k in range(0, span_at, 256):
-                        ks = slice(k, k + 256)
-                        cols = pl.ds(pl.multiple_of(at * span_at + k, 256), 256)
-                        a = lax.dot_general(
-                            full[:, ks], green[flat, cols], NT, preferred_element_type=F32
-                        )
-                        b = jnp.dot(green[long, cols], tall[ks, :], preferred_element_type=F32)
-                        wide_out = a if wide_out is None else wide_out + a
-                        long_out = b if long_out is None else long_out + b
-                    target[:, flat] = target[:, flat] + wide_out
-                    target[:, long] = target[:, long] + long_out.T
+            @pl.when(i + 1 < batches)
+            def _():
+                collect(i + 1)
+
+            for start in range(0, npix, 1024):
+                flat = slice(start, start + 512)
+                long = slice(start + 512, start + 1024)
+                wide_out = long_out = None
+                for k in range(0, span_at, 256):
+                    ks = slice(k, k + 256)
+                    cols = pl.ds(pl.multiple_of(at * span_at + k, 256), 256)
+                    a = lax.dot_general(
+                        full[:, ks], green[flat, cols], NT, preferred_element_type=F32
+                    )
+                    b = jnp.dot(green[long, cols], tall[ks, :], preferred_element_type=F32)
+                    wide_out = a if wide_out is None else wide_out + a
+                    long_out = b if long_out is None else long_out + b
+                target[:, flat] = target[:, flat] + wide_out
+                target[:, long] = target[:, long] + long_out.T
 
         settle(gath, 2 * each - 1 + (batches - 1) * each, s_g)
         settle(gath, (batches - 1) * each, s_f)
@@ -680,24 +675,6 @@
     slip = slip + project(part_b, r_pb, pair_b, r_hb, False)[0] / bound
     slip_ref[...] = slip
     share(slip, gath_b, r_gb, r_fb, pred_ref)
-
-
-def relay(pred_ref, slip_ref, pred_out, slip_out, pred_buf, slip_buf, sems):
-    rows = 8
-    count = pred_ref.shape[0] // rows
-    moves = [(slip_ref, slip_buf, slip_out)]
-    for i in range(count):
-        at = pl.ds(i * rows, rows)
-        moves.append((pred_ref.at[at], pred_buf.at[at], pred_out.at[at]))
-    loads = [pltpu.make_async_copy(a, b, sems.at[0, i]) for i, (a, b, c) in enumerate(moves)]
-    stores = [pltpu.make_async_copy(b, c, sems.at[1, i]) for i, (a, b, c) in enumerate(moves)]
-    for load in loads:
-        load.start()
-    for load, store in zip(loads, stores):
-        load.wait()
-        store.start()
-    for store in stores:
-        store.wait()
 
 
 def on_device(interferograms, epoch_pairs, los, patch_place, patch_depth):
@@ -735,8 +712,8 @@
     predicted, slip = pl.pallas_call(
         functools.partial(kernel, cfg),
         out_shape=(
-            jax.ShapeDtypeStruct((NEP, npix), F32),
-            jax.ShapeDtypeStruct((NEP, LANES), F32),
+            pltpu.VMEM((NEP, npix), F32),
+            pltpu.VMEM((NEP, LANES), F32),
         ),
         in_specs=[vmem, vmem, vmem, vmem, pl.BlockSpec(memory_space=pl.ANY)],
         out_specs=(vmem, vmem),
@@ -791,21 +768,9 @@
             dma((batches,)),
         ],
         compiler_params=pltpu.CompilerParams(
-            collective_id=0, has_side_effects=True, vmem_limit_bytes=62 * 1024 * 1024
+            collective_id=0, has_side_effects=True, vmem_limit_bytes=59 * 1024 * 1024
         ),
     )(epoch_pairs, los, patch_place, patch_depth[None], xs)
-    anywhere = pl.BlockSpec(memory_space=pl.ANY)
-    predicted, slip = pl.pallas_call(
-        relay,
-        out_shape=tuple(jax.ShapeDtypeStruct(a.shape, F32) for a in (predicted, slip)),
-        in_specs=[anywhere, anywhere],
-        out_specs=(anywhere, anywhere),
-        scratch_shapes=[
-            pltpu.VMEM(predicted.shape, F32),
-            pltpu.VMEM(slip.shape, F32),
-            dma((2, 1 + NEP // 8)),
-        ],
-    )(predicted, slip)
     if reps > 1:
         slip = lax.dynamic_slice_in_dim(slip, (me % reps) * own, own, 1)
     return (predicted, slip)

time: 105 us -> 104 us (level)
  Pallas kernels: 104 us -> 101 us
  local copies, waits for them, and re-layouts: 0 us -> 1.59 us
    pallas_call x2 -> x1, Pallas kernels: 104 us -> 101 us  [on_device(): pl.pallas_call(functools.partial(kernel, cfg), out_shape=(pltpu.VMEM((NEP...]
    unnamed x0 -> x2, local copies, waits for them, and re-layouts: none -> 1.59 us
where the time goes in v4:
time: 104 us; the launch traced here: 103 us
  Pallas kernels  101 us (97%)
  local copies, waits for them, and re-layouts  1.59 us (2%)
    pallas_call x1, Pallas kernels, on_device(): pl.pallas_call(functools.partial(kernel, cfg), out_shape=(pltpu.VMEM((NEP...  101 us

profile of v4, /device:TPU:0, one launch (start us, length us, event | category | flops | bytes accessed | tf_op | source)
XLA Modules:
  0.0 103.5 jit_solution(7621646920938455103)
XLA Ops:
  0.6 101.3 %shard_map.68 = (f32[64,4096]{1,0:T(8,128)S(1)}, f32[64,128]{1,0:T(8,128)S(1)}) custom-call(s32[2,256]{1,0:T(2,128)} %pairs_ref.1, f32[3,4096]{1,0:T(4,128)} %los_ref.1, s32[2,4096]{1,0:T(2,128)} %place_ref.1, s32[1,4096]{1,0:T(1,128)} %bitcast.1, f32[8,131072]{1,0:T(8,128)} %xs_ref.1), custom_call_target="tpu_custom_call" | custom-call | tf_op jit(solution)/shard_map/pallas_call | solution.py:712
  101.9 1.0 copy.9
  102.9 0.6 copy.10

commit v5 on v4

--- a/solution.py
+++ b/solution.py
@@ -262,11 +262,11 @@
             row = row + brow[:, cols]
         brow[:, cols] = row
 
-    def generate(line):
-        if line > 0:
+    def generate(line, first, last):
+        if line > 0 and first == 0:
             weigh(line - 1)
 
-        @pl.loop(0, per_line)
+        @pl.loop(first, last)
         def _(t):
             if line > 0:
                 gather_bound(line - 1, t)
@@ -278,6 +278,7 @@
                 if (line + 1) * per_line * turns <= swept:
                     sweep((line * per_line + t) * turns + q)
             total = jnp.zeros((strip, LANES), F32)
+            held = None
             for c in range(npatch // wide):
                 num = jnp.dot(
                     mix, basis[:, c * wide : (c + 1) * wide], preferred_element_type=F32
@@ -288,9 +289,18 @@
                     away = xpos - prow[0:1, at]
                     inv = lax.rsqrt(away * away + prow[1 + line : 2 + line, at])
                     g = num[:, j * LANES : (j + 1) * LANES] * (inv * inv * inv)
-                    total = total + jnp.abs(g)
                     halves.append(g.astype(BF16))
+                size = jnp.abs(halves[0])
+                for piece in halves[1:]:
+                    size = size + jnp.abs(piece)
+                if held is None:
+                    held = size
+                else:
+                    total = total + (held + size).astype(F32)
+                    held = None
                 green[pl.ds(start, strip), c * wide : (c + 1) * wide] = jnp.concatenate(halves, 1)
+            if held is not None:
+                total = total + held.astype(F32)
             wacc[pl.ds(start, strip), :] = total
 
     def invert():
@@ -342,7 +352,15 @@
     ready = min(lines, -(-NEP // (per_line * turns)))
     halved = 0
     for line in range(lines):
-        generate(line)
+        pause = per_line * 3 // 4
+        if chunks > 1 and line == lines - 1 and ready <= line:
+            generate(line, 0, pause)
+            for c in range(halved, chunks):
+                halve(c)
+            halved = chunks
+            generate(line, pause, per_line)
+        else:
+            generate(line, 0, per_line)
         if line == ready - 1:
             pieces = invert()
         if chunks > 1 and line >= ready - 1:

time: 104 us -> 104 us (level)
  no operation moved by 1% of the time
where the time goes in v5:
time: 104 us; the launch traced here: 103 us
  Pallas kernels  101 us (97%)
  local copies, waits for them, and re-layouts  1.59 us (2%)
    pallas_call x1, Pallas kernels, on_device(): pl.pallas_call(functools.partial(kernel, cfg), out_shape=(pltpu.VMEM((NEP...  101 us

profile of v5, /device:TPU:0, one launch (start us, length us, event | category | flops | bytes accessed | tf_op | source)
XLA Modules:
  0.0 103.3 jit_solution(12583689615807429806)
XLA Ops:
  0.6 101.1 %shard_map.68 = (f32[64,4096]{1,0:T(8,128)S(1)}, f32[64,128]{1,0:T(8,128)S(1)}) custom-call(s32[2,256]{1,0:T(2,128)} %pairs_ref.1, f32[3,4096]{1,0:T(4,128)} %los_ref.1, s32[2,4096]{1,0:T(2,128)} %place_ref.1, s32[1,4096]{1,0:T(1,128)} %bitcast.1, f32[8,131072]{1,0:T(8,128)} %xs_ref.1), custom_call_target="tpu_custom_call" | custom-call | tf_op jit(solution)/shard_map/pallas_call | solution.py:730
  101.7 1.0 copy.9
  102.7 0.6 copy.10
